TPU v7x, 256 devices: a 4x2x16 block of a 4x16x16 slice. The times are simulated.
256 devices in a mesh: pb: 2 (over y), col: 32 (over z, core), row: 4 (over x).
Axes of the slice: x: 4, y: 2, z: 16, core: 2. Of those that a mesh axis runs over, the one named last changes fastest.
The devices are a block of a 4x16x16 slice.
Arguments:
- pair_density: bfloat16 [6144, 6144], P(('pb', 'col'), 'row'), parts along dimension 0, may hold values from -0.19921875 to 0.19921875
- band_pairs: int32 [2, 3072], replicated, may hold values from 0 to 255, as said below
- valence: float32 [256], replicated, may hold values from -12 to -2
- conduction: float32 [12], replicated, may hold values from 1 to 8
- wave_vectors: int32 [3, 12288], P(None, 'pb'), parts along dimension 1, may hold values from -6 to 6
- momentum: float32 [6], P('pb'), parts along dimension 0, may hold values from 0.3 to 0.7
- guess_scale: float32 [12288], P('pb'), parts along dimension 0, may hold values from 0.4 to 0.75
Outputs:
- epsilon: float32 [12288, 6144], P(('pb', 'row'), 'col'), parts along dimension 0
- inverse: float32 [12288, 6144], P(('pb', 'row'), 'col'), parts along dimension 0
There are 2 independent parts, one for each index of `pb`. A program takes and returns all parts, laid end to end along the dimension named above; an argument that names none is the same for every part. Nothing has to cross between parts.
Inputs may be any that keep to these rules, and one draw needn't show every extreme that they name: `band_pairs`: column p names a valence band below 256 in row 0 and a conduction band below 12 in row 1; every such pair of bands appears in exactly one column.
All inputs are finite; a program needn't handle non-finite values.
Results may differ from a plain program's by a relative error of at most 0.0036.
The roundings to bfloat16 on the way count: a program that leaves them out, or rounds other values in their place, can miss the bound.
Values may be sent and summed in bfloat16 or wider, within the bound.
No kernel may reach another device: no remote copies, remote signals or barrier semaphores. Data moves between devices by JAX's collectives and lax.ppermute only.
A program may use at most 64 MiB of HBM per device.

v0:
```python
import math
import jax
import jax.numpy as jnp
from jax import lax
from jax.sharding import PartitionSpec as P


def copy_for_each(array, axis):
    copies = jnp.broadcast_to(array, (lax.axis_size(axis), *array.shape))
    return lax.all_to_all(copies, axis, split_axis=0, concat_axis=0, tiled=True)


def in_order(pieces, dim):
    lengths = list(pieces.shape[1:])
    lengths[dim] *= pieces.shape[0]
    return jnp.moveaxis(pieces, 0, dim).reshape(lengths)


def gathered_copies(array, axis, dim):
    pieces = copy_for_each(array, axis)
    return in_order(pieces, dim)


def lookup(indices, table):
    levels = jnp.arange(table.shape[0], dtype=jnp.int32)
    picked = indices[:, None] == levels[None, :]
    return jnp.sum(jnp.where(picked, table[None, :], 0.0), axis=1)


def on_device(pair_density, band_pairs, valence, conduction, wave_vectors, momentum, guess_scale):
    column_index = lax.axis_index("col")
    row_index = lax.axis_index("row")
    row_height = pair_density.shape[1]
    whole_width = row_height * lax.axis_size("row")
    strip_width = whole_width // lax.axis_size("col")
    valence_of = lookup(band_pairs[0], valence)
    conduction_of = lookup(band_pairs[1], conduction)
    weight = 4.0 / (valence_of - conduction_of)
    shifted = wave_vectors.astype(jnp.float32) + momentum[:, None]
    sqrt_all = jnp.sqrt(4.0 * math.pi / jnp.sum(shifted * shifted, axis=0))
    row_first = row_index * row_height
    column_first = column_index * strip_width
    sqrt_rows = lax.dynamic_slice_in_dim(sqrt_all, row_first, row_height, 0)
    sqrt_cols = lax.dynamic_slice_in_dim(sqrt_all, column_first, strip_width, 0)
    scale_rows = lax.dynamic_slice_in_dim(guess_scale, row_first, row_height, 0)
    scale_cols = lax.dynamic_slice_in_dim(guess_scale, column_first, strip_width, 0)
    panel_pairs = lax.all_gather(pair_density, "col", axis=0, tiled=True)
    owner = column_first // row_height
    offset = column_first % row_height
    own_slice = lax.dynamic_slice_in_dim(panel_pairs, offset, strip_width, 1)
    candidates = lax.all_gather(own_slice, "row", axis=1, tiled=True)
    strip_pairs = lax.dynamic_slice_in_dim(candidates, owner * strip_width, strip_width, 1)
    weighted = (weight[:, None] * panel_pairs.astype(jnp.float32)).astype(jnp.bfloat16)
    weighted_strip = (weight[:, None] * strip_pairs.astype(jnp.float32)).astype(jnp.bfloat16)
    chi_block = lax.dot_general(
        weighted, strip_pairs, (((0,), (0,)), ((), ())), preferred_element_type=jnp.float32
    )
    chi_rows = jnp.sum(weighted.astype(jnp.float32) * panel_pairs.astype(jnp.float32), axis=0)
    chi_cols = jnp.sum(weighted_strip.astype(jnp.float32) * strip_pairs.astype(jnp.float32), axis=0)
    global_rows = row_first + jnp.arange(row_height, dtype=jnp.int32)
    global_cols = column_first + jnp.arange(strip_width, dtype=jnp.int32)
    identity = (global_rows[:, None] == global_cols[None, :]).astype(jnp.float32)
    epsilon = identity - sqrt_rows[:, None] * chi_block * sqrt_cols[None, :]
    guess_rows = scale_rows / (1.0 - sqrt_rows * chi_rows * sqrt_rows)
    guess_cols = scale_cols / (1.0 - sqrt_cols * chi_cols * sqrt_cols)
    mixed = epsilon * guess_cols[None, :]
    mixed_b = mixed.astype(jnp.bfloat16)
    panel_mixed = lax.all_gather(mixed_b, "col", axis=1, tiled=True)
    strip_mixed = gathered_copies(mixed_b, "row", 0)
    square = jnp.dot(panel_mixed, strip_mixed, preferred_element_type=jnp.float32)
    square_b = square.astype(jnp.bfloat16)
    strip_square = gathered_copies(square_b, "row", 0)
    cube = jnp.dot(panel_mixed, strip_square, preferred_element_type=jnp.float32)
    inverse = guess_rows[:, None] * (4.0 * identity - 6.0 * mixed + 4.0 * square - cube)
    return (epsilon, inverse)


def solution(mesh):
    placed = (P(("pb", "col"), "row"), P(), P(), P(), P(None, "pb"), P("pb"), P("pb"))
    return jax.shard_map(
        on_device,
        mesh=mesh,
        in_specs=placed,
        out_specs=(P(("pb", "row"), "col"), P(("pb", "row"), "col")),
        check_vma=False,
    )
```

profile of v0, /device:TPU:33, one launch (start us, length us, event | category | flops | bytes accessed | tf_op | source)
XLA Modules:
  0.0 345.0 jit_solution(10228950458131673058)
XLA Ops:
  7.2 0.1 all-gather.4.cloned.1.call-start
  7.2 0.7 all-gather.4.cloned.1.call-update
  8.0 0.1 all-gather.6.cloned.1.call-start
  8.1 94.8 %all-gather.4.cloned.1.call-done = bf16[3072,1536]{1,0:T(8,128)(2,1)} async-done(((bf16[96,1536]{1,0:T(8,128)(2,1)}), bf16[3072,1536]{1,0:T(8,128)(2,1)}) %all-gather.4.cloned.1.call-update) | async-done | bytes 9437200 | tf_op jit(solution)/shard_map/all_gather | solution.py:47
  102.8 2.4 constant_dynamic-slice_fusion
  105.3 0.0 copy-start.1
  105.3 0.0 copy-start.4
  105.3 0.0 copy-start
  105.3 0.0 copy-start.3
  105.3 0.0 copy-start.2
  105.3 1.5 copy.18
  106.8 0.1 all-gather.6.cloned.1.call-update
  106.9 0.1 all-gather.8.cloned.1.call-start
  107.0 0.0 copy-done.1
  107.0 0.0 copy-done.4
  107.0 0.1 select_reduce_fusion.1
  107.1 0.0 copy-done
  107.2 0.0 copy-done.3
  107.2 0.1 multiply_reduce_fusion
  107.3 0.0 copy-done.2
  107.3 1.9 select_reduce_fusion
  109.2 6.2 %fusion.1 = f32[1536]{0:T(1024)S(1)} fusion(bf16[3072,1536]{1,0:T(8,128)(2,1)} %all-gather.4.cloned.1.call-done, f32[3072]{0:T(1024)S(1)} %subtract_divide_fusion), kind=kLoop, calls=%fused_computation.3 | loop fusion | flops 28310016 | bytes 9455616 | tf_op jit(solution)/shard_map/reduce_sum | solution.py:58
  115.5 0.8 fusion.20
  116.3 44.8 %all-gather.6.cloned.1.call-done = bf16[3072,768]{0,1:T(8,128)(2,1)} async-done(((bf16[3072,192]{0,1:T(8,128)(2,1)}), bf16[3072,768]{0,1:T(8,128)(2,1)}) %all-gather.6.cloned.1.call-update) | async-done | bytes 4718608 | tf_op jit(solution)/shard_map/all_gather | solution.py:51
  161.0 1.7 fusion.15
  162.7 0.8 fusion.22
  163.5 7.6 %multiply_convert_fusion = (bf16[1536,192]{0,1:T(8,128)(2,1)}, f32[1536,192]{0,1:T(8,128)}) fusion(f32[192]{0:T(256)S(1)} %get-tuple-element.4, f32[192]{0:T(256)S(1)} %get-tuple-element.5, bf16[3072,1536]{1,0:T(8,128)(2,1)} %all-gather.4.cloned.1.call-done, f32[3072]{0:T(1024)S(1)} %subtract_divide_fusion, ...), kind=kOutput, calls=%fused_computation.20 | convolution fusion | flops 1828159488 | bytes 12413188 | tf_op jit(solution)/shard_map/dot_general | solution.py:55
  171.1 0.1 all-gather.8.cloned.1.call-update
  171.2 1.2 broadcast_in_dim.47
  172.4 31.0 %all_to_all.10 = bf16[4,1536,192]{1,2,0:T(8,128)(2,1)S(1)} all-to-all(bf16[4,1536,192]{1,2,0:T(8,128)(2,1)S(1)} %broadcast_in_dim.47), channel_id=1, replica_groups=mesh['pb'=2,'col'=32,'row'=4] {'row'}, dimensions={0} | all-to-all | bytes 4718592 | tf_op jit(solution)/shard_map/all_to_all | solution.py:10
  203.5 0.3 copy.21
  203.7 84.0 %all-gather.8.cloned.1.call-done = bf16[1536,6144]{0,1:T(8,128)(2,1)} async-done(((bf16[1536,192]{0,1:T(8,128)(2,1)}), bf16[1536,6144]{0,1:T(8,128)(2,1)}) %all-gather.8.cloned.1.call-update) | async-done | bytes 18874384 | tf_op jit(solution)/shard_map/all_gather | solution.py:68
  287.8 0.0 slice-start
  287.8 0.0 slice-start.1
  287.8 0.0 slice-start.2
  287.8 11.4 %fusion.25 = (bf16[1536,192]{0,1:T(8,128)(2,1)S(1)}, f32[1536,192]{0,1:T(8,128)}) fusion(bf16[6144,192]{0,1:T(8,128)(2,1)S(1)} %bitcast.13, bf16[1536,6144]{0,1:T(8,128)(2,1)} %all-gather.8.cloned.1.call-done), kind=kOutput, calls=%fused_computation.38 | convolution fusion | flops 3624173568 | bytes 23003136 | tf_op jit(solution)/shard_map/dot_general | solution.py:70
  299.1 0.2 broadcast_in_dim.48
  299.3 0.0 slice-start.4
  299.3 32.6 %all_to_all.11 = bf16[4,1536,192]{1,2,0:T(8,128)(2,1)S(1)} all-to-all(bf16[4,1536,192]{1,2,0:T(8,128)(2,1)S(1)} %broadcast_in_dim.48), channel_id=1, replica_groups=mesh['pb'=2,'col'=32,'row'=4] {'row'}, dimensions={0} | all-to-all | bytes 4718592 | tf_op jit(solution)/shard_map/all_to_all | solution.py:10
  331.9 0.3 copy.22
  332.2 0.0 slice-done
  332.2 0.0 slice-done.1
  332.2 0.0 slice-done.2
  332.2 0.0 slice-done.3
  332.2 0.0 slice-done.4
  332.2 1.0 copy-done.5
  333.2 0.4 copy-done.6
  333.6 4.9 %fusion.13 = f32[1536,192]{0,1:T(8,128)} fusion(bf16[6144,192]{0,1:T(8,128)(2,1)S(1)} %bitcast.12, bf16[1536,6144]{0,1:T(8,128)(2,1)S(1)} %bitcast.17, f32[1536,192]{0,1:T(8,128)S(1)} %copy-done.6, f32[1536,192]{0,1:T(8,128)S(1)} %copy-done.5, f32[192]{0:T(256)S(1)} %get-tuple-element.4, f32[1536]{0:T(1024)S(1)} %get-tuple-element.2, ...), kind=kOutput, calls=%fused_computation.13 | convolution fusion | flops 3626532864 | bytes 24786432 | tf_op jit(solution)/shard_map/dot_general | solution.py:73
  (9 shorter events, 0.1 us)
Async XLA Ops:
  7.2 95.7 %all-gather.4.cloned.1.call-start = ((), (), s32[]{:S(2)}) async-start(), calls=%async_computation.2 | async-start | bytes 9732096 | tf_op jit(solution)/shard_map/all_gather | solution.py:47
  8.0 153.0 %all-gather.6.cloned.1.call-start = ((), (), s32[]{:S(2)}) async-start(), calls=%async_computation.3 | async-start | bytes 5898240 | tf_op jit(solution)/shard_map/all_gather | solution.py:51
  105.3 1.7 copy-start.1
  105.3 1.7 copy-start.4
  105.3 1.9 copy-start
  105.3 1.9 copy-start.3
  105.3 2.0 copy-start.2
  106.9 180.9 %all-gather.8.cloned.1.call-start = ((), (), s32[]{:S(2)}) async-start(), calls=%async_computation.4 | async-start | bytes 19464192 | tf_op jit(solution)/shard_map/all_gather | solution.py:68
  287.8 44.4 %slice-start = ((s8[18874368]{0:T(1024)(128)(4,1)}), s8[4194304]{0:T(1024)(128)(4,1)S(1)}, s32[]{:S(2)}) async-start(s8[18874368]{0:T(1024)(128)(4,1)} %bitcast.16), calls=%async_computation.5 | async-start | bytes 8388608
  287.8 44.4 %slice-start.1 = ((s8[18874368]{0:T(1024)(128)(4,1)}), s8[4194304]{0:T(1024)(128)(4,1)S(1)}, s32[]{:S(2)}) async-start(s8[18874368]{0:T(1024)(128)(4,1)} %bitcast.16), calls=%async_computation.6 | async-start | bytes 8388608
  287.8 44.5 %slice-start.2 = ((s8[18874368]{0:T(1024)(128)(4,1)}), s8[4194304]{0:T(1024)(128)(4,1)S(1)}, s32[]{:S(2)}) async-start(s8[18874368]{0:T(1024)(128)(4,1)} %bitcast.16), calls=%async_computation.7 | async-start | bytes 8388608
  287.8 44.5 %slice-start.3 = ((s8[18874368]{0:T(1024)(128)(4,1)}), s8[4194304]{0:T(1024)(128)(4,1)S(1)}, s32[]{:S(2)}) async-start(s8[18874368]{0:T(1024)(128)(4,1)} %bitcast.16), calls=%async_computation.8 | async-start | bytes 8388608
  299.3 32.9 %slice-start.4 = ((s8[18874368]{0:T(1024)(128)(4,1)}), s8[2097152]{0:T(1024)(128)(4,1)S(1)}, s32[]{:S(2)}) async-start(s8[18874368]{0:T(1024)(128)(4,1)} %bitcast.16), calls=%async_computation.9 | async-start | bytes 4194304
  331.9 1.3 copy-start.5
  331.9 1.6 copy-start.6
Sparse Core Ops, SparseCore 0:
  9.9 92.9 all-gather.3
  107.0 53.9 all-gather.5
  171.3 116.4 all-gather.7
where the time goes:
time: 346 us; the launch traced here: 345 us
  waiting for transfers between devices  224 us (65%)
  blocking collectives  63.7 us (18%)
  matrix products  23.9 us (7%)
  between operations  14.1 us (4%)
  other arithmetic  11.6 us (3%)
  local copies, waits for them, and re-layouts  7.24 us (2%)
    all_gather x1, waiting for transfers between devices, on_device(): panel_pairs = lax.all_gather(pair_density, 'col', axis=0, tiled=True)  94.8 us
    all_gather x1, waiting for transfers between devices, on_device(): panel_mixed = lax.all_gather(mixed_b, 'col', axis=1, tiled=True)  84 us
    all_to_all x2, blocking collectives, copy_for_each(): return lax.all_to_all(copies, axis, split_axis=0, concat_axis=0, tiled=True)  63.7 us
    all_gather x1, waiting for transfers between devices, on_device(): candidates = lax.all_gather(own_slice, 'row', axis=1, tiled=True)  44.8 us
    dot_general x1, matrix products, on_device(): jnp.dot(panel_mixed, strip_mixed, preferred_element_type=jnp.float32)  11.4 us
    dot_general x1, matrix products, on_device(): lax.dot_general(weighted, strip_pairs, (((0,), (0,)), ((), ())), preferre...  7.63 us
  transfers between devices with their start and end apart: 3, of which 3 were waited for; matrix products, arithmetic and copies ran while one was open for 3% of the time, Pallas kernels for 0%

commit v1 on v0

--- a/solution.py
+++ b/solution.py
@@ -1,8 +1,19 @@
+import functools
 import math
 import jax
 import jax.numpy as jnp
 from jax import lax
 from jax.sharding import PartitionSpec as P
+
+
+def create_page(here_x, along_axis):
+    opened = jnp.stack([here_x for _ in range(lax.axis_size(along_axis))])
+    piece_now = lax.all_to_all(opened, along_axis, 0, 0)
+    moved = jnp.concatenate(piece_now, axis=0)
+    return moved
+
+
+return_all_the_pages = functools.partial(create_page, along_axis="col")
 
 
 def copy_for_each(array, axis):
@@ -44,7 +55,7 @@
     sqrt_cols = lax.dynamic_slice_in_dim(sqrt_all, column_first, strip_width, 0)
     scale_rows = lax.dynamic_slice_in_dim(guess_scale, row_first, row_height, 0)
     scale_cols = lax.dynamic_slice_in_dim(guess_scale, column_first, strip_width, 0)
-    panel_pairs = lax.all_gather(pair_density, "col", axis=0, tiled=True)
+    panel_pairs = return_all_the_pages(pair_density)
     owner = column_first // row_height
     offset = column_first % row_height
     own_slice = lax.dynamic_slice_in_dim(panel_pairs, offset, strip_width, 1)

time: 346 us -> 694 us (2.01)
  waiting for transfers between devices: 224 us -> 541 us
  starting transfers between devices: 0.19 us -> 25.6 us
    all_to_all x0 -> x1, waiting for transfers between devices: none -> 403 us  [create_page(): piece_now = lax.all_to_all(opened, along_axis, 0, 0)]
    all_gather x1 -> x0, waiting for transfers between devices: 94.8 us -> none  [on_device(): panel_pairs = lax.all_gather(pair_density, 'col', axis=0, tiled=True)]
    all_to_all x0 -> x1, starting transfers between devices: none -> 25.5 us  [create_page(): piece_now = lax.all_to_all(opened, along_axis, 0, 0)]
    all_gather x1, waiting for transfers between devices: 44.8 us -> 53.6 us  [on_device(): candidates = lax.all_gather(own_slice, 'row', axis=1, tiled=True)]
  transfers between devices with their start and end apart: 3 -> 3, of which waited for: 3 -> 3; matrix products, arithmetic and copies ran while one was open for 3% -> 2% of each run, Pallas kernels for 0% -> 0%
where the time goes in v1:
time: 694 us; the launch traced here: 693 us
  waiting for transfers between devices  541 us (78%)
  blocking collectives  63.7 us (9%)
  starting transfers between devices  25.6 us (4%)
  matrix products  23.9 us (3%)
  between operations  14.3 us (2%)
  local copies, waits for them, and re-layouts  13 us (2%)
  other arithmetic  11.6 us (2%)
    all_to_all x1, waiting for transfers between devices, create_page(): piece_now = lax.all_to_all(opened, along_axis, 0, 0)  403 us
    all_gather x1, waiting for transfers between devices, on_device(): panel_mixed = lax.all_gather(mixed_b, 'col', axis=1, tiled=True)  84 us
    all_to_all x2, blocking collectives, copy_for_each(): return lax.all_to_all(copies, axis, split_axis=0, concat_axis=0, tiled=True)  63.7 us
    all_gather x1, waiting for transfers between devices, on_device(): candidates = lax.all_gather(own_slice, 'row', axis=1, tiled=True)  53.6 us
    all_to_all x1, starting transfers between devices, create_page(): piece_now = lax.all_to_all(opened, along_axis, 0, 0)  25.5 us
  transfers between devices with their start and end apart: 3, of which 3 were waited for; matrix products, arithmetic and copies ran while one was open for 2% of the time, Pallas kernels for 0%

profile of v1, /device:TPU:33, one launch (start us, length us, event | category | flops | bytes accessed | tf_op | source)
XLA Modules:
  0.0 693.0 jit_solution(7609673548336638979)
XLA Ops:
  7.2 5.7 stack.2
  12.9 25.5 %all-to-all-start = ((bf16[32,96,1536]{2,1,0:T(8,128)(2,1)}), bf16[32,96,1536]{2,1,0:T(8,128)(2,1)}, u32[]{:S(2)}, u32[]{:S(2)}) async-start(bf16[32,96,1536]{2,1,0:T(8,128)(2,1)} %stack.2), calls=%async_computation | async-start | bytes 18874368 | tf_op jit(solution)/shard_map/all_to_all | solution.py:11
  38.3 0.1 all-gather.3.cloned.1.call-start
  38.4 403.2 %all-to-all-done = bf16[32,96,1536]{2,1,0:T(8,128)(2,1)} async-done(((bf16[32,96,1536]{2,1,0:T(8,128)(2,1)}), bf16[32,96,1536]{2,1,0:T(8,128)(2,1)}, u32[]{:S(2)}, u32[]{:S(2)}) %all-to-all-start) | async-done | bytes 9437216 | tf_op jit(solution)/shard_map/all_to_all | solution.py:11
  441.6 2.4 constant_dynamic-slice_fusion
  444.0 0.0 copy-start.1
  444.0 0.0 copy-start.4
  444.0 0.0 copy-start.2
  444.1 0.0 copy-start
  444.1 0.0 copy-start.3
  444.1 1.5 copy.15
  445.6 0.1 all-gather.3.cloned.1.call-update
  445.6 0.1 all-gather.5.cloned.1.call-start
  445.7 0.0 copy-done.1
  445.8 0.0 copy-done.4
  445.8 0.1 select_reduce_fusion.1
  445.9 0.0 copy-done.2
  445.9 1.9 select_reduce_fusion
  447.8 0.1 div.35
  447.9 0.0 copy-done
  447.9 0.0 copy-done.3
  447.9 0.1 multiply_reduce_fusion
  448.1 6.2 fusion.1
  454.3 0.8 fusion.14
  455.1 53.6 %all-gather.3.cloned.1.call-done = bf16[3072,768]{0,1:T(8,128)(2,1)} async-done(((bf16[3072,192]{0,1:T(8,128)(2,1)}), bf16[3072,768]{0,1:T(8,128)(2,1)}) %all-gather.3.cloned.1.call-update) | async-done | bytes 4718608 | tf_op jit(solution)/shard_map/all_gather | solution.py:62
  508.7 1.7 fusion.9
  510.3 0.8 fusion.16
  511.1 7.7 %multiply_convert_fusion.8 = (bf16[1536,192]{0,1:T(8,128)(2,1)}, f32[1536,192]{0,1:T(8,128)}) fusion(f32[192]{0:T(256)S(1)} %get-tuple-element.4, f32[192]{0:T(256)S(1)} %get-tuple-element.5, bf16[3072,1536]{1,0:T(8,128)(2,1)} %bitcast.2, f32[3072]{0:T(1024)S(1)} %subtract_divide_fusion, bf16[3072,768]{0,1:T(8,128)(2,1)} %all-gather.3.cloned.1.call-done, ...), kind=kOutput, calls=%fused_computation.22 | convolution fusion | flops 1828159488 | bytes 12413188 | tf_op jit(solution)/shard_map/dot_general | solution.py:66
  518.8 0.1 all-gather.5.cloned.1.call-update
  518.8 1.2 broadcast_in_dim.47
  520.1 31.1 %all_to_all.15 = bf16[4,1536,192]{1,2,0:T(8,128)(2,1)S(1)} all-to-all(bf16[4,1536,192]{1,2,0:T(8,128)(2,1)S(1)} %broadcast_in_dim.47), channel_id=1, replica_groups=mesh['pb'=2,'col'=32,'row'=4] {'row'}, dimensions={0} | all-to-all | bytes 4718592 | tf_op jit(solution)/shard_map/all_to_all | solution.py:21
  551.2 0.3 copy.18
  551.4 84.0 %all-gather.5.cloned.1.call-done = bf16[1536,6144]{0,1:T(8,128)(2,1)} async-done(((bf16[1536,192]{0,1:T(8,128)(2,1)}), bf16[1536,6144]{0,1:T(8,128)(2,1)}) %all-gather.5.cloned.1.call-update) | async-done | bytes 18874384 | tf_op jit(solution)/shard_map/all_gather | solution.py:79
  635.4 0.0 slice-start
  635.4 0.0 slice-start.1
  635.4 11.4 %fusion.19 = (bf16[1536,192]{0,1:T(8,128)(2,1)S(1)}, f32[1536,192]{0,1:T(8,128)}) fusion(bf16[6144,192]{0,1:T(8,128)(2,1)S(1)} %bitcast.14, bf16[1536,6144]{0,1:T(8,128)(2,1)} %all-gather.5.cloned.1.call-done), kind=kOutput, calls=%fused_computation.40 | convolution fusion | flops 3624173568 | bytes 23003136 | tf_op jit(solution)/shard_map/dot_general | solution.py:81
  646.8 0.2 broadcast_in_dim.48
  647.0 0.0 slice-start.4
  647.0 32.6 %all_to_all.16 = bf16[4,1536,192]{1,2,0:T(8,128)(2,1)S(1)} all-to-all(bf16[4,1536,192]{1,2,0:T(8,128)(2,1)S(1)} %broadcast_in_dim.48), channel_id=1, replica_groups=mesh['pb'=2,'col'=32,'row'=4] {'row'}, dimensions={0} | all-to-all | bytes 4718592 | tf_op jit(solution)/shard_map/all_to_all | solution.py:21
  679.6 0.3 copy.19
  679.8 0.0 slice-done
  679.8 0.0 slice-done.1
  679.9 0.0 slice-done.2
  679.9 0.0 slice-done.3
  679.9 0.0 slice-done.4
  679.9 1.0 copy-done.5
  680.8 0.4 copy-done.6
  681.2 4.9 fusion.7
  (10 shorter events, 0.1 us)
Async XLA Ops:
  12.9 428.7 %all-to-all-start = ((bf16[32,96,1536]{2,1,0:T(8,128)(2,1)}), bf16[32,96,1536]{2,1,0:T(8,128)(2,1)}, u32[]{:S(2)}, u32[]{:S(2)}) async-start(bf16[32,96,1536]{2,1,0:T(8,128)(2,1)} %stack.2), calls=%async_computation | async-start | bytes 18874368 | tf_op jit(solution)/shard_map/all_to_all | solution.py:11
  38.3 470.3 %all-gather.3.cloned.1.call-start = ((), (), s32[]{:S(2)}) async-start(), calls=%async_computation.3 | async-start | bytes 5898240 | tf_op jit(solution)/shard_map/all_gather | solution.py:62
  444.0 1.7 copy-start.1
  444.0 1.7 copy-start.4
  444.0 1.8 copy-start.2
  444.1 3.8 copy-start
  444.1 3.8 copy-start.3
  445.6 189.8 %all-gather.5.cloned.1.call-start = ((), (), s32[]{:S(2)}) async-start(), calls=%async_computation.4 | async-start | bytes 19464192 | tf_op jit(solution)/shard_map/all_gather | solution.py:79
  635.4 44.4 %slice-start = ((s8[18874368]{0:T(1024)(128)(4,1)}), s8[4194304]{0:T(1024)(128)(4,1)S(1)}, s32[]{:S(2)}) async-start(s8[18874368]{0:T(1024)(128)(4,1)} %bitcast.17), calls=%async_computation.5 | async-start | bytes 8388608
  635.4 44.4 %slice-start.1 = ((s8[18874368]{0:T(1024)(128)(4,1)}), s8[4194304]{0:T(1024)(128)(4,1)S(1)}, s32[]{:S(2)}) async-start(s8[18874368]{0:T(1024)(128)(4,1)} %bitcast.17), calls=%async_computation.6 | async-start | bytes 8388608
  635.4 44.5 %slice-start.2 = ((s8[18874368]{0:T(1024)(128)(4,1)}), s8[4194304]{0:T(1024)(128)(4,1)S(1)}, s32[]{:S(2)}) async-start(s8[18874368]{0:T(1024)(128)(4,1)} %bitcast.17), calls=%async_computation.7 | async-start | bytes 8388608
  635.4 44.5 %slice-start.3 = ((s8[18874368]{0:T(1024)(128)(4,1)}), s8[4194304]{0:T(1024)(128)(4,1)S(1)}, s32[]{:S(2)}) async-start(s8[18874368]{0:T(1024)(128)(4,1)} %bitcast.17), calls=%async_computation.8 | async-start | bytes 8388608
  647.0 32.9 %slice-start.4 = ((s8[18874368]{0:T(1024)(128)(4,1)}), s8[2097152]{0:T(1024)(128)(4,1)S(1)}, s32[]{:S(2)}) async-start(s8[18874368]{0:T(1024)(128)(4,1)} %bitcast.17), calls=%async_computation.9 | async-start | bytes 4194304
  679.6 1.3 copy-start.5
  679.6 1.6 copy-start.6
Sparse Core Ops, SparseCore 0:
  445.7 62.8 all-gather.2
  518.9 116.4 all-gather.4
